TPU v7x, 32 devices: a whole 2x2x4 slice. The times are simulated.
32 devices in a mesh: strip: 32 (over z, y, x, core).
Axes of the slice: x: 2, y: 2, z: 4, core: 2. Of those that a mesh axis runs over, the one named last changes fastest.
Arguments:
- features: bfloat16 [64, 1024, 1024], P(None, 'strip'), may hold values from -6 to 6
- row_kernel: bfloat16 [8, 8, 8, 129], replicated, may hold values from -0.1875 to 0.1875
- mix_weight: bfloat16 [64, 64], replicated, may hold values from -0.75 to 0.75
- channel_bias: float32 [64], replicated, may hold values from -3 to 3
Outputs:
- layer_out: bfloat16 [64, 1024, 1024], P(None, 'strip')
All inputs are finite; a program needn't handle non-finite values.
Results may differ from a plain program's by a relative error of at most 0.001.
Values may be sent and summed in bfloat16 or wider, within the bound.
A program may use at most 128 MiB of HBM per device.

v0:
```python
import functools

import jax
import jax.numpy as jnp
from jax import lax
from jax.experimental import pallas as pl
from jax.experimental.pallas import tpu as pltpu
from jax.sharding import PartitionSpec as P

MESH = pl.DeviceIdType.MESH
CORES = 2
PIECES = 2
AHEAD = 2


def kernel(
    chips,
    features,
    taps,
    mixes,
    bias,
    out,
    own,
    halo,
    weights,
    mixer,
    total,
    staged,
    own_sem,
    own_send,
    own_recv,
    near_send,
    near_recv,
    far_send,
    far_recv,
    out_sem,
    out_send,
    out_recv,
):
    channels, strip_rows, columns = features.shape
    groups, segments, width, lanes = taps.shape
    part = columns // CORES
    piece = part // PIECES
    block = width * strip_rows

    me = lax.axis_index("strip")
    chip, core = lax.div(me, CORES), lax.rem(me, CORES)
    odd = lax.rem(chip, 2)
    near_chip = chip + 1 - 2 * odd
    far_chip = lax.rem(chip + 2 + odd * (chips - 4), chips)
    back_chip = lax.rem(chip + (chips - 2) - odd * (chips - 4), chips)
    peer = chip * CORES + 1 - core
    far = far_chip * CORES + core
    back = back_chip * CORES + core

    def half(which):
        return pl.ds(pl.multiple_of(which * part, part), part)

    def group_rows(g):
        return pl.ds(pl.multiple_of(g * width, width), width)

    def own_load():
        return pltpu.make_async_copy(features.at[:, :, half(core)], own.at[core], own_sem)

    def own_swap():
        return pltpu.make_async_remote_copy(
            src_ref=features.at[:, :, half(1 - core)],
            dst_ref=own.at[core],
            send_sem=own_send,
            recv_sem=own_recv,
            device_id=(peer,),
            device_id_type=MESH,
        )

    def near_copy(g, q, target):
        return pltpu.make_async_remote_copy(
            src_ref=features.at[group_rows(g), :, pl.ds(target * part + q * piece, piece)],
            dst_ref=halo.at[odd, core, group_rows(g), :, pl.ds(q * piece, piece)],
            send_sem=near_send,
            recv_sem=near_recv.at[g, q, core],
            device_id=(near_chip * CORES + target,),
            device_id_type=MESH,
        )

    def near_wait(g, q, t):
        region = halo.at[1 - odd, t, group_rows(g), :, pl.ds(q * piece, piece)]
        pltpu.make_async_remote_copy(
            src_ref=region,
            dst_ref=region,
            send_sem=near_send,
            recv_sem=near_recv.at[g, q, t],
            device_id=(far,),
            device_id_type=MESH,
        ).wait_recv()

    def far_copy(g, q, t):
        return pltpu.make_async_remote_copy(
            src_ref=halo.at[1 - odd, t, group_rows(g), :, pl.ds(q * piece, piece)],
            dst_ref=halo.at[odd, t, group_rows(g), :, pl.ds(q * piece, piece)],
            send_sem=far_send,
            recv_sem=far_recv.at[g, q, t],
            device_id=(far,),
            device_id_type=MESH,
        )

    def send_near(g):
        for q in range(PIECES):
            for target in range(CORES):
                near_copy(g, q, target).start()

    def relay(g, q):
        for t in range(CORES):
            near_wait(g, q, t)
            far_copy(g, q, t).start()

    def build(g):
        shape = (strip_rows, 128)
        row = lax.broadcasted_iota(jnp.int32, shape, 0)
        lane = lax.rem(lax.broadcasted_iota(jnp.int32, shape, 1), strip_rows)
        inside = lane >= row
        same = lane == row
        for o in range(width):
            rows = pl.ds(o * strip_rows, strip_rows)
            for first in range(0, lanes, 128):
                before = jnp.zeros(shape, jnp.float32)
                for s in range(segments):
                    line = jnp.broadcast_to(taps[g, s, pl.ds(o, 1), pl.ds(first, 128)], shape)
                    here = pltpu.roll(line, 0, 1, stride=1, stride_axis=0)
                    weights[s, rows, pl.ds(first, 128)] = jnp.where(inside, here, before).astype(jnp.bfloat16)
                    before = pltpu.roll(line, 128 - strip_rows, 1, stride=1, stride_axis=0)
            for first in range(0, channels * strip_rows, 128):
                line = jnp.broadcast_to(mixes[g, pl.ds(o, 1), pl.ds(first, 128)], shape)
                mixer[rows, pl.ds(first, 128)] = jnp.where(same, line, 0.0).astype(jnp.bfloat16)

    def dot(a, b):
        return jnp.dot(a, b, preferred_element_type=jnp.float32)

    def inner(g):
        for q in range(PIECES):
            cols = pl.ds(q * piece, piece)
            for b in range(CORES):
                value = None
                for t in range(CORES):
                    term = dot(weights[t - b + 2], own[t, group_rows(g), :, cols].reshape(block, piece))
                    value = term if value is None else value + term
                for i in range(groups):
                    value += dot(
                        mixer[:, pl.ds(i * block, block)],
                        own[b, pl.ds(i * width, width), :, cols].reshape(block, piece),
                    )
                total[b, :, cols] = value

    def outer(g, q):
        cols = pl.ds(q * piece, piece)
        for t in range(CORES):
            far_copy(g, q, t).wait_recv()
        for b in range(CORES):
            value = total[b, :, cols]
            for role in range(2):
                for t in range(CORES):
                    s = t + (2 * CORES if role else 0) - b
                    if 0 <= s < segments:
                        value += dot(weights[s], halo[role, t, group_rows(g), :, cols].reshape(block, piece))
            for o in range(width):
                x = value[o * strip_rows : (o + 1) * strip_rows] + bias[g * width + o]
                staged[b, g * width + o, :, cols] = jax.nn.gelu(x).astype(jnp.bfloat16)
        place = pl.ds(pl.multiple_of(core * part + q * piece, piece), piece)
        pltpu.make_async_copy(
            staged.at[core, group_rows(g), :, cols], out.at[group_rows(g), :, place], out_sem
        ).start()
        pltpu.make_async_remote_copy(
            src_ref=staged.at[1 - core, group_rows(g), :, cols],
            dst_ref=out.at[group_rows(g), :, place],
            send_sem=out_send,
            recv_sem=out_recv,
            device_id=(peer,),
            device_id_type=MESH,
        ).start()

    own_load().start()
    barrier = pltpu.get_barrier_semaphore()
    friends = (peer, near_chip * CORES, near_chip * CORES + 1, far, back)
    for friend in friends:
        pl.semaphore_signal(barrier, inc=1, device_id=(friend,), device_id_type=MESH)
    pl.semaphore_wait(barrier, len(friends))

    for g in range(AHEAD):
        send_near(g)
    own_swap().start()
    own_load().wait()
    own_swap().wait_recv()

    def step(g, carry):
        @pl.when(g + AHEAD < groups)
        def _():
            send_near(g + AHEAD)

        relay(g, 0)

        @pl.when(g > 0)
        def _():
            for q in range(PIECES):
                outer(g - 1, q)

        for q in range(1, PIECES):
            relay(g, q)
        build(g)
        inner(g)
        return carry

    lax.fori_loop(0, groups, step, 0)
    for q in range(PIECES):
        outer(groups - 1, q)

    own_swap().wait_send()
    everything = pltpu.make_async_remote_copy(
        src_ref=features,
        dst_ref=features,
        send_sem=near_send,
        recv_sem=out_recv,
        device_id=(peer,),
        device_id_type=MESH,
    )
    everything.wait_send()
    pltpu.make_async_remote_copy(
        src_ref=halo.at[0],
        dst_ref=halo.at[1],
        send_sem=far_send,
        recv_sem=out_recv,
        device_id=(peer,),
        device_id_type=MESH,
    ).wait_send()
    pltpu.make_async_copy(staged.at[core], out.at[:, :, half(core)], out_sem).wait()
    swapped = pltpu.make_async_remote_copy(
        src_ref=staged.at[1 - core],
        dst_ref=out.at[:, :, half(1 - core)],
        send_sem=out_send,
        recv_sem=out_recv,
        device_id=(peer,),
        device_id_type=MESH,
    )
    swapped.wait_send()
    swapped.wait_recv()


def local(chips, features, row_kernel, mix_weight, channel_bias):
    channels, strip_rows, columns = features.shape
    groups, width, _, tap_count = row_kernel.shape
    assert tap_count - 1 == 2 * CORES * strip_rows
    segments = 2 * CORES + 1
    part = columns // CORES
    block = width * strip_rows
    taps = jnp.pad(row_kernel, ((0, 0), (0, 0), (0, 0), (0, segments * strip_rows - tap_count)))
    taps = taps.reshape(groups, width, width, segments, strip_rows)
    taps = taps.transpose(0, 3, 1, 2, 4).reshape(groups, segments, width, block)
    taps = taps.astype(jnp.float32)
    mixes = jnp.repeat(mix_weight.T.astype(jnp.float32), strip_rows, axis=1)
    mixes = mixes.reshape(groups, width, channels * strip_rows)
    dma = pltpu.SemaphoreType.DMA
    bf16 = features.dtype
    return pl.pallas_call(
        functools.partial(kernel, chips),
        name="layer",
        out_shape=jax.ShapeDtypeStruct(features.shape, bf16),
        in_specs=[
            pl.BlockSpec(memory_space=pl.ANY),
            pl.BlockSpec(memory_space=pltpu.VMEM),
            pl.BlockSpec(memory_space=pltpu.VMEM),
            pl.BlockSpec(memory_space=pltpu.SMEM),
        ],
        out_specs=pl.BlockSpec(memory_space=pl.ANY),
        scratch_shapes=[
            pltpu.VMEM((CORES, channels, strip_rows, part), bf16),
            pltpu.VMEM((2, CORES, channels, strip_rows, part), bf16),
            pltpu.VMEM((segments, block, block), bf16),
            pltpu.VMEM((block, channels * strip_rows), bf16),
            pltpu.VMEM((CORES, block, part), jnp.float32),
            pltpu.VMEM((CORES, channels, strip_rows, part), bf16),
            dma,
            dma,
            dma,
            dma,
            dma((groups, PIECES, CORES)),
            dma,
            dma((groups, PIECES, CORES)),
            dma,
            dma,
            dma,
        ],
        compiler_params=pltpu.CompilerParams(
            collective_id=0, has_side_effects=True, vmem_limit_bytes=48 * 1024 * 1024
        ),
    )(features, taps, mixes, channel_bias)


def solution(mesh):
    chips = mesh.shape["strip"] // CORES
    assert chips % 2 == 0 and chips >= 4
    return jax.shard_map(
        functools.partial(local, chips),
        mesh=mesh,
        in_specs=(P(None, "strip", None), P(), P(), P()),
        out_specs=P(None, "strip", None),
        check_vma=False,
    )
```

profile of v0, /device:TPU:0, one launch (start us, length us, event | category | flops | bytes accessed | tf_op | source)
XLA Modules:
  0.0 112.8 jit_solution(14569033619246232289)
XLA Ops:
  0.0 0.7 convert_bitcast_fusion
  0.7 0.1 copy.8
  0.8 1.0 pad_convert_fusion
  1.8 0.3 reshape.7
  2.1 0.0 copy-start
  2.1 0.2 copy.7
  2.4 0.4 reshape.6.taps
  2.8 0.6 broadcast_in_dim.3
  3.4 1.0 reshape_reshape.3.mixes
  4.3 0.0 copy-done
  4.3 106.4 %layer.1 = bf16[64,32,1024]{2,1,0:T(8,128)(2,1)S(1)} custom-call(bf16[64,32,1024]{2,1,0:T(8,128)(2,1)} %features.1, f32[8,5,8,256]{3,2,1,0:T(8,128)S(1)} %reshape.6.taps, f32[8,8,2048]{2,1,0:T(8,128)S(1)} %reshape_reshape.3.mixes, f32[64]{0:T(128)S(1)} %copy-done), custom_call_target="tpu_custom_call" | custom-call | tf_op jit(solution)/shard_map/layer/pallas_call | solution.py:261
  110.8 2.0 %copy.10 = bf16[64,32,1024]{2,1,0:T(8,128)(2,1)} copy(bf16[64,32,1024]{2,1,0:T(8,128)(2,1)S(1)} %layer.1) | data formatting | bytes 8388608
Async XLA Ops:
  2.1 2.2 %copy-start = (f32[64]{0:T(128)S(1)}, f32[64]{0:T(128)}, u32[]{:S(2)}) copy-start(f32[64]{0:T(128)} %bias.1) | copy-start | bytes 772
where the time goes:
time: 113 us
  Pallas kernels  106 us (94%)
  local copies, waits for them, and re-layouts  4.6 us (4%)
  other arithmetic  1.72 us (2%)
    pallas_call x1, Pallas kernels, local(): pl.pallas_call(functools.partial(kernel, chips), name='layer', out_shape=...  106 us

commit v1 on v0

v1 whole, which is shorter than its diff:
```python
import functools

import jax
import jax.numpy as jnp
from jax import lax
from jax.experimental import pallas as pl
from jax.experimental.pallas import tpu as pltpu
from jax.sharding import PartitionSpec as P

MESH = pl.DeviceIdType.MESH
CORES = 2
LANES = 128
PAIR = 2
AHEAD = 2


def kernel(
    chips,
    features,
    row_kernel,
    mix_weight,
    channel_bias,
    out,
    own,
    other,
    halo,
    raw,
    raw_mix,
    bias,
    spread,
    taps,
    mixes,
    weights,
    mixer,
    total,
    staged,
    load_sem,
    param_sem,
    own_send,
    own_recv,
    near_send,
    near_recv,
    far_send,
    far_recv,
    out_sem,
    out_send,
    out_recv,
):
    groups, width, strip_rows, columns = features.shape
    _, _, _, pieces, _, _, piece = halo.shape
    segments = weights.shape[1]
    tap_count = row_kernel.shape[1]
    part = columns // CORES
    block = width * strip_rows
    pairs = pieces // PAIR
    span = PAIR * piece

    me = lax.axis_index("strip")
    chip, core = lax.div(me, CORES), lax.rem(me, CORES)
    odd = lax.rem(chip, 2)
    near_chip = chip + 1 - 2 * odd
    far_chip = lax.rem(chip + 2 + odd * (chips - 4), chips)
    back_chip = lax.rem(chip + (chips - 2) - odd * (chips - 4), chips)
    peer = chip * CORES + 1 - core
    far = far_chip * CORES + core
    back = back_chip * CORES + core
    near = (near_chip * CORES + core, near_chip * CORES + 1 - core)

    def half(which):
        return pl.ds(pl.multiple_of(which * part, part), part)

    def load(g):
        for mine, which in ((own.at[core], core), (other, 1 - core)):
            for q in range(pieces):
                place = pl.ds(pl.multiple_of(which * part + q * piece, piece), piece)
                pltpu.make_async_copy(features.at[g, :, :, place], mine.at[g, q], load_sem.at[g]).start()

    def loaded(g):
        pltpu.make_async_copy(features.at[g], features.at[g], load_sem.at[g]).wait()

    def swap(g):
        return pltpu.make_async_remote_copy(
            src_ref=other.at[g],
            dst_ref=own.at[core, g],
            send_sem=own_send,
            recv_sem=own_recv,
            device_id=(peer,),
            device_id_type=MESH,
        )

    def near_copy(g, q, turn):
        return pltpu.make_async_remote_copy(
            src_ref=other.at[g, q] if turn else own.at[core, g, q],
            dst_ref=halo.at[odd, core, g, q],
            send_sem=near_send,
            recv_sem=near_recv.at[g, q, turn],
            device_id=(near[turn],),
            device_id_type=MESH,
        )

    def far_copy(g, q, turn):
        t = 1 - core if turn else core
        return pltpu.make_async_remote_copy(
            src_ref=halo.at[1 - odd, t, g, q],
            dst_ref=halo.at[odd, t, g, q],
            send_sem=far_send,
            recv_sem=far_recv.at[g, q, turn],
            device_id=(far,),
            device_id_type=MESH,
        )

    def near_wait(g, q, turn):
        region = halo.at[1 - odd, 1 - core if turn else core, g, q]
        pltpu.make_async_remote_copy(
            src_ref=region,
            dst_ref=region,
            send_sem=near_send,
            recv_sem=near_recv.at[g, q, turn],
            device_id=(far,),
            device_id_type=MESH,
        ).wait_recv()

    def send_near(g):
        for q in range(pieces):
            for turn in range(2):
                near_copy(g, q, turn).start()

    def relay(g, q):
        for turn in range(2):
            near_wait(g, q, turn)
            far_copy(g, q, turn).start()

    def dot(a, b):
        return jnp.dot(a, b, preferred_element_type=jnp.float32)

    def prepare():
        rows = groups * width
        raw_copy.wait()
        mix_copy.wait()
        bias_copy.wait()
        spread[...] = jnp.zeros_like(spread)
        for page in range(spread.shape[0]):
            size = min(LANES, tap_count - page * LANES)
            spread[page, :, pl.ds(0, size)] = raw[:, pl.ds(page * LANES, size)].astype(jnp.float32)
        fit = LANES // strip_rows
        lane = lax.broadcasted_iota(jnp.int32, (rows, LANES), 1)
        for first in range(0, width, fit):
            for s in range(segments):
                line = jnp.zeros((rows, LANES), jnp.float32)
                for n in range(fit):
                    source = pl.ds(first + n, rows, stride=width)
                    part_line = spread[s * strip_rows // LANES, source, :]
                    shift = (n * strip_rows - s * strip_rows) % LANES
                    part_line = pltpu.roll(part_line, shift, 1) if shift else part_line
                    line = jnp.where(lane // strip_rows == n, part_line, line)
                taps[s, :, :, pl.ds(first * strip_rows, LANES)] = line.reshape(groups, width, LANES)
        shape = (rows, rows * strip_rows)
        pick = lax.broadcasted_iota(jnp.int32, shape, 1) // strip_rows == lax.broadcasted_iota(jnp.int32, shape, 0)
        expanded = lax.dot_general(
            raw_mix[...],
            pick.astype(raw_mix.dtype),
            (((0,), (0,)), ((), ())),
            preferred_element_type=jnp.float32,
        )
        mixes[...] = expanded.reshape(mixes.shape)

    def build(g):
        slot = lax.rem(g, 2)
        shape = (strip_rows, LANES)
        row = lax.broadcasted_iota(jnp.int32, shape, 0)
        lane = lax.rem(lax.broadcasted_iota(jnp.int32, shape, 1), strip_rows)
        inside = lane >= row
        same = lane == row
        for o in range(width):
            rows = pl.ds(o * strip_rows, strip_rows)
            source = pl.ds(o, 1)
            for first in range(0, block, LANES):
                before = jnp.zeros(shape, jnp.float32)
                for s in range(segments):
                    line = jnp.broadcast_to(taps[s, g, source, pl.ds(first, LANES)], shape)
                    here = pltpu.roll(line, 0, 1, stride=1, stride_axis=0)
                    weights[lax.rem(g, 3), s, rows, pl.ds(first, LANES)] = jnp.where(inside, here, before).astype(jnp.bfloat16)
                    before = pltpu.roll(line, LANES - strip_rows, 1, stride=1, stride_axis=0)
            for first in range(0, groups * block, LANES):
                line = jnp.broadcast_to(mixes[g, source, pl.ds(first, LANES)], shape)
                mixer[rows, pl.ds(first, LANES)] = jnp.where(same, line, 0.0).astype(jnp.bfloat16)

    def wide(ref, n):
        return jnp.concatenate([ref[n * PAIR + k].reshape(block, piece) for k in range(PAIR)], axis=1)

    def inner(g):
        slot = lax.rem(g, 2)
        for n in range(pairs):
            for b in range(CORES):
                value = None
                for t in range(CORES):
                    term = dot(weights[lax.rem(g, 3), t - b + CORES], wide(own.at[t, g], n))
                    value = term if value is None else value + term
                for i in range(groups):
                    value += dot(mixer[:, pl.ds(i * block, block)], wide(own.at[b, i], n))
                total[slot, b, :, pl.ds(n * span, span)] = value

    def outer(g, n):
        slot = lax.rem(g, 2)
        cols = pl.ds(n * span, span)
        for q in range(n * PAIR, (n + 1) * PAIR):
            for turn in range(2):
                far_copy(g, q, turn).wait_recv()
        for b in range(CORES):
            value = total[slot, b, :, cols]
            for role in range(2):
                for t in range(CORES):
                    s = t + (2 * CORES if role else 0) - b
                    if 0 <= s < segments:
                        value += dot(weights[lax.rem(g, 3), s], wide(halo.at[role, t, g], n))
            for o in range(width):
                x = value[o * strip_rows : (o + 1) * strip_rows] + bias[g * width + o]
                staged[b, g, o, :, cols] = jax.nn.gelu(x).astype(jnp.bfloat16)
        place = pl.ds(pl.multiple_of(core * part + n * span, span), span)
        pltpu.make_async_copy(staged.at[core, g, :, :, cols], out.at[g, :, :, place], out_sem).start()
        pltpu.make_async_remote_copy(
            src_ref=staged.at[1 - core, g, :, :, cols],
            dst_ref=out.at[g, :, :, place],
            send_sem=out_send,
            recv_sem=out_recv,
            device_id=(peer,),
            device_id_type=MESH,
        ).start()

    for g in range(AHEAD):
        load(g)
    barrier = pltpu.get_barrier_semaphore()
    friends = (peer, *near, far, back)
    for friend in friends:
        pl.semaphore_signal(barrier, inc=1, device_id=(friend,), device_id_type=MESH)
    raw_copy = pltpu.make_async_copy(row_kernel, raw, param_sem.at[0])
    mix_copy = pltpu.make_async_copy(mix_weight, raw_mix, param_sem.at[1])
    bias_copy = pltpu.make_async_copy(channel_bias, bias, param_sem.at[2])
    for g in range(AHEAD, groups):
        load(g)
    raw_copy.start()
    mix_copy.start()
    bias_copy.start()
    pl.semaphore_wait(barrier, len(friends))

    for g in range(AHEAD):
        loaded(g)
        send_near(g)
        swap(g).start()
    for g in range(AHEAD, groups):
        loaded(g)
        swap(g).start()
    prepare()
    pltpu.make_async_remote_copy(
        src_ref=other,
        dst_ref=own.at[1 - core],
        send_sem=own_send,
        recv_sem=own_recv,
        device_id=(peer,),
        device_id_type=MESH,
    ).wait_recv()

    def step(g, carry):
        @pl.when(g + AHEAD < groups)
        def _():
            send_near(g + AHEAD)

        relay(g, 0)

        @pl.when(g == 0)
        def _():
            build(g)
            inner(g)

        @pl.when(g + 1 < groups)
        def _():
            build(g + 1)

        relay(g, 1)

        @pl.when(g > 0)
        def _():
            outer(g - 1, 1)

        relay(g, 2)

        @pl.when(g + 1 < groups)
        def _():
            inner(g + 1)

        relay(g, 3)
        outer(g, 0)
        return carry

    lax.fori_loop(0, groups, step, 0)
    outer(groups - 1, 1)

    def sent(ref, sem):
        pltpu.make_async_remote_copy(
            src_ref=ref,
            dst_ref=ref,
            send_sem=sem,
            recv_sem=out_recv,
            device_id=(peer,),
            device_id_type=MESH,
        ).wait_send()

    sent(other, own_send)
    sent(features, near_send)
    sent(halo.at[0], far_send)
    pltpu.make_async_copy(staged.at[core], out.at[:, :, :, half(core)], out_sem).wait()
    swapped = pltpu.make_async_remote_copy(
        src_ref=staged.at[1 - core],
        dst_ref=out.at[:, :, :, half(1 - core)],
        send_sem=out_send,
        recv_sem=out_recv,
        device_id=(peer,),
        device_id_type=MESH,
    )
    swapped.wait_send()
    swapped.wait_recv()


def fixed(array):
    return pltpu.with_memory_space_constraint(array, pltpu.HBM)


def local(chips, features, row_kernel, mix_weight, channel_bias):
    channels, strip_rows, columns = features.shape
    groups, width, _, tap_count = row_kernel.shape
    assert tap_count - 1 == 2 * CORES * strip_rows and LANES % strip_rows == 0
    segments = 2 * CORES + 1
    part = columns // CORES
    block = width * strip_rows
    pieces = part // LANES
    assert pieces == 4
    dma = pltpu.SemaphoreType.DMA
    bf16 = features.dtype
    shape = (groups, width, strip_rows, columns)
    buffer = (groups, pieces, width, strip_rows, LANES)
    anywhere = pl.BlockSpec(memory_space=pl.ANY)
    out = pl.pallas_call(
        functools.partial(kernel, chips),
        name="layer",
        out_shape=jax.ShapeDtypeStruct(shape, bf16),
        in_specs=[pl.BlockSpec(memory_space=pltpu.HBM)] * 4,
        out_specs=anywhere,
        scratch_shapes=[
            pltpu.VMEM((CORES, *buffer), bf16),
            pltpu.VMEM(buffer, bf16),
            pltpu.VMEM((2, CORES, *buffer), bf16),
            pltpu.VMEM((channels * width, tap_count), row_kernel.dtype),
            pltpu.VMEM((channels, channels), mix_weight.dtype),
            pltpu.SMEM((channels,), channel_bias.dtype),
            pltpu.VMEM((pl.cdiv(tap_count, LANES), channels * width, LANES), jnp.float32),
            pltpu.VMEM((segments, groups, width, block), jnp.float32),
            pltpu.VMEM((groups, width, channels * strip_rows), jnp.float32),
            pltpu.VMEM((3, segments, block, block), bf16),
            pltpu.VMEM((block, channels * strip_rows), bf16),
            pltpu.VMEM((2, CORES, block, part), jnp.float32),
            pltpu.VMEM((CORES, groups, width, strip_rows, part), bf16),
            dma((groups,)),
            dma((3,)),
            dma,
            dma,
            dma,
            dma((groups, pieces, CORES)),
            dma,
            dma((groups, pieces, CORES)),
            dma,
            dma,
            dma,
        ],
        compiler_params=pltpu.CompilerParams(
            collective_id=0, has_side_effects=True, vmem_limit_bytes=48 * 1024 * 1024
        ),
    )(
        features.reshape(shape),
        fixed(row_kernel.reshape(channels * width, tap_count)),
        fixed(mix_weight),
        fixed(channel_bias),
    )
    return out.reshape(features.shape)


def solution(mesh):
    chips = mesh.shape["strip"] // CORES
    assert chips % 2 == 0 and chips >= 4
    return jax.shard_map(
        functools.partial(local, chips),
        mesh=mesh,
        in_specs=(P(None, "strip", None), P(), P(), P()),
        out_specs=P(None, "strip", None),
        check_vma=False,
    )
```

time: 113 us -> 108 us (0.956)
  local copies, waits for them, and re-layouts: 4.6 us -> 2.02 us
  other arithmetic: 1.72 us -> 0 us
    convert_element_type x2 -> x0, other arithmetic: 1.72 us -> none  [the longest x1 1 us: local(): taps = taps.astype(jnp.float32)]
where the time goes in v1:
time: 108 us
  Pallas kernels  106 us (98%)
  local copies, waits for them, and re-layouts  2.02 us (2%)
    pallas_call x1, Pallas kernels, local(): pl.pallas_call(functools.partial(kernel, chips), name='layer', out_shape=...  106 us

profile of v1, /device:TPU:0, one launch (start us, length us, event | category | flops | bytes accessed | tf_op | source)
XLA Modules:
  0.0 107.8 jit_solution(7200534660285493524)
XLA Ops:
  0.0 105.8 %layer.1 = bf16[8,8,32,1024]{3,2,1,0:T(8,128)(2,1)S(1)} custom-call(bf16[8,8,32,1024]{3,2,1,0:T(8,128)(2,1)} %bitcast.4, bf16[512,129]{1,0:T(8,128)(2,1)} %bitcast.5, bf16[64,64]{1,0:T(8,128)(2,1)} %mix_weight.1, f32[64]{0:T(128)} %channel_bias.1), custom_call_target="tpu_custom_call" | custom-call | tf_op jit(solution)/shard_map/layer/pallas_call | solution.py:342
  105.8 2.0 %copy.6 = bf16[64,32,1024]{2,1,0:T(8,128)(2,1)} copy(bf16[64,32,1024]{2,1,0:T(8,128)(2,1)S(1)} %bitcast.3) | data formatting | bytes 8388608

commit v2 on v1

--- a/solution.py
+++ b/solution.py
@@ -34,6 +34,7 @@
     mixer,
     total,
     staged,
+    stage,
     load_sem,
     param_sem,
     own_send,
@@ -45,6 +46,9 @@
     out_sem,
     out_send,
     out_recv,
+    hop_send,
+    hop_recv,
+    ready,
 ):
     groups, width, strip_rows, columns = features.shape
     _, _, _, pieces, _, _, piece = halo.shape
@@ -63,8 +67,11 @@
     back_chip = lax.rem(chip + (chips - 2) - odd * (chips - 4), chips)
     peer = chip * CORES + 1 - core
     far = far_chip * CORES + core
-    back = back_chip * CORES + core
     near = (near_chip * CORES + core, near_chip * CORES + 1 - core)
+    back = (back_chip * CORES + core, back_chip * CORES + 1 - core)
+    up_chip = lax.rem(chip + 2, chips)
+    down_chip = lax.rem(chip + chips - 2, chips)
+    last = (groups - 1, pieces - 1)
 
     def half(which):
         return pl.ds(pl.multiple_of(which * part, part), part)
@@ -120,6 +127,26 @@
             device_id_type=MESH,
         ).wait_recv()
 
+    def hop_copy(turn):
+        return pltpu.make_async_remote_copy(
+            src_ref=other.at[last] if turn else own.at[core, *last],
+            dst_ref=stage.at[turn],
+            send_sem=hop_send,
+            recv_sem=hop_recv.at[turn],
+            device_id=(back[turn],),
+            device_id_type=MESH,
+        )
+
+    def hop_forward(turn):
+        return pltpu.make_async_remote_copy(
+            src_ref=stage.at[turn],
+            dst_ref=halo.at[1 - odd, 1 - core if turn else core, *last],
+            send_sem=far_send,
+            recv_sem=far_recv.at[*last, turn],
+            device_id=(near[0],),
+            device_id_type=MESH,
+        )
+
     def send_near(g):
         for q in range(pieces):
             for turn in range(2):
@@ -128,7 +155,10 @@
     def relay(g, q):
         for turn in range(2):
             near_wait(g, q, turn)
-            far_copy(g, q, turn).start()
+            if q < last[1]:
+                far_copy(g, q, turn).start()
+            else:
+                pl.when(g < last[0])(far_copy(g, q, turn).start)
 
     def dot(a, b):
         return jnp.dot(a, b, preferred_element_type=jnp.float32)
@@ -185,8 +215,8 @@
                 line = jnp.broadcast_to(mixes[g, source, pl.ds(first, LANES)], shape)
                 mixer[rows, pl.ds(first, LANES)] = jnp.where(same, line, 0.0).astype(jnp.bfloat16)
 
-    def wide(ref, n):
-        return jnp.concatenate([ref[n * PAIR + k].reshape(block, piece) for k in range(PAIR)], axis=1)
+    def wide(ref, first, count):
+        return jnp.concatenate([ref[first + k].reshape(block, piece) for k in range(count)], axis=1)
 
     def inner(g):
         slot = lax.rem(g, 2)
@@ -194,16 +224,16 @@
             for b in range(CORES):
                 value = None
                 for t in range(CORES):
-                    term = dot(weights[lax.rem(g, 3), t - b + CORES], wide(own.at[t, g], n))
+                    term = dot(weights[lax.rem(g, 3), t - b + CORES], wide(own.at[t, g], n * PAIR, PAIR))
                     value = term if value is None else value + term
                 for i in range(groups):
-                    value += dot(mixer[:, pl.ds(i * block, block)], wide(own.at[b, i], n))
+                    value += dot(mixer[:, pl.ds(i * block, block)], wide(own.at[b, i], n * PAIR, PAIR))
                 total[slot, b, :, pl.ds(n * span, span)] = value
 
-    def outer(g, n):
+    def outer(g, first, count):
         slot = lax.rem(g, 2)
-        cols = pl.ds(n * span, span)
-        for q in range(n * PAIR, (n + 1) * PAIR):
+        cols = pl.ds(first * piece, count * piece)
+        for q in range(first, first + count):
             for turn in range(2):
                 far_copy(g, q, turn).wait_recv()
         for b in range(CORES):
@@ -212,11 +242,11 @@
                 for t in range(CORES):
                     s = t + (2 * CORES if role else 0) - b
                     if 0 <= s < segments:
-                        value += dot(weights[lax.rem(g, 3), s], wide(halo.at[role, t, g], n))
+                        value += dot(weights[lax.rem(g, 3), s], wide(halo.at[role, t, g], first, count))
             for o in range(width):
                 x = value[o * strip_rows : (o + 1) * strip_rows] + bias[g * width + o]
                 staged[b, g, o, :, cols] = jax.nn.gelu(x).astype(jnp.bfloat16)
-        place = pl.ds(pl.multiple_of(core * part + n * span, span), span)
+        place = pl.ds(pl.multiple_of(core * part + first * piece, piece), count * piece)
         pltpu.make_async_copy(staged.at[core, g, :, :, cols], out.at[g, :, :, place], out_sem).start()
         pltpu.make_async_remote_copy(
             src_ref=staged.at[1 - core, g, :, :, cols],
@@ -227,28 +257,49 @@
             device_id_type=MESH,
         ).start()
 
-    for g in range(AHEAD):
-        load(g)
+    load(0)
+    load(groups - 1)
     barrier = pltpu.get_barrier_semaphore()
-    friends = (peer, *near, far, back)
-    for friend in friends:
+    close = (*near, peer, down_chip * CORES, down_chip * CORES + 1)
+    above = (up_chip * CORES, up_chip * CORES + 1)
+    for friend in close:
         pl.semaphore_signal(barrier, inc=1, device_id=(friend,), device_id_type=MESH)
+
+    @pl.when(chip < chips - 2)
+    def _():
+        for friend in above:
+            pl.semaphore_signal(barrier, inc=1, device_id=(friend,), device_id_type=MESH)
+
     raw_copy = pltpu.make_async_copy(row_kernel, raw, param_sem.at[0])
     mix_copy = pltpu.make_async_copy(mix_weight, raw_mix, param_sem.at[1])
     bias_copy = pltpu.make_async_copy(channel_bias, bias, param_sem.at[2])
-    for g in range(AHEAD, groups):
+    for g in range(1, groups - 1):
         load(g)
     raw_copy.start()
     mix_copy.start()
     bias_copy.start()
-    pl.semaphore_wait(barrier, len(friends))
-
-    for g in range(AHEAD):
+    pl.semaphore_wait(barrier, len(close) + len(above) * jnp.minimum(lax.div(chip, 2), 1))
+
+    @pl.when(chip >= chips - 2)
+    def _():
+        for friend in above:
+            pl.semaphore_signal(ready, inc=1, device_id=(friend,), device_id_type=MESH)
+
+
+    def hop():
+        for turn in range(2):
+            hop_copy(turn).start()
+
+    loaded(0)
+    send_near(0)
+    loaded(groups - 1)
+    pl.when(chip > 0)(hop)
+    for g in range(1, AHEAD):
         loaded(g)
         send_near(g)
-        swap(g).start()
-    for g in range(AHEAD, groups):
+    for g in range(AHEAD, groups - 1):
         loaded(g)
+    for g in range(groups):
         swap(g).start()
     prepare()
     pltpu.make_async_remote_copy(
@@ -260,7 +311,22 @@
         device_id_type=MESH,
     ).wait_recv()
 
+    @pl.when(chip == 1)
+    def _():
+        pl.semaphore_wait(ready, len(above))
+
     def step(g, carry):
+        @pl.when((g == 1) & (chip == 0))
+        def _():
+            pl.semaphore_wait(ready, len(above))
+            hop()
+
+        @pl.when(g == groups - 1)
+        def _():
+            for turn in range(2):
+                hop_copy(turn).wait_recv()
+                hop_forward(turn).start()
+
         @pl.when(g + AHEAD < groups)
         def _():
             send_near(g + AHEAD)
@@ -280,7 +346,7 @@
 
         @pl.when(g > 0)
         def _():
-            outer(g - 1, 1)
+            outer(g - 1, PAIR, PAIR)
 
         relay(g, 2)
 
@@ -289,11 +355,12 @@
             inner(g + 1)
 
         relay(g, 3)
-        outer(g, 0)
+        outer(g, 0, PAIR)
         return carry
 
     lax.fori_loop(0, groups, step, 0)
-    outer(groups - 1, 1)
+    for q in reversed(range(PAIR, pieces)):
+        outer(groups - 1, q, 1)
 
     def sent(ref, sem):
         pltpu.make_async_remote_copy(
@@ -308,6 +375,7 @@
     sent(other, own_send)
     sent(features, near_send)
     sent(halo.at[0], far_send)
+    sent(stage, hop_send)
     pltpu.make_async_copy(staged.at[core], out.at[:, :, :, half(core)], out_sem).wait()
     swapped = pltpu.make_async_remote_copy(
         src_ref=staged.at[1 - core],
@@ -359,6 +427,7 @@
             pltpu.VMEM((block, channels * strip_rows), bf16),
             pltpu.VMEM((2, CORES, block, part), jnp.float32),
             pltpu.VMEM((CORES, groups, width, strip_rows, part), bf16),
+            pltpu.VMEM((2, width, strip_rows, LANES), bf16),
             dma((groups,)),
             dma((3,)),
             dma,
@@ -370,6 +439,9 @@
             dma,
             dma,
             dma,
+            dma,
+            dma((2,)),
+            pltpu.SemaphoreType.REGULAR,
         ],
         compiler_params=pltpu.CompilerParams(
             collective_id=0, has_side_effects=True, vmem_limit_bytes=48 * 1024 * 1024

time: 108 us -> 105 us (0.972)
  Pallas kernels: 106 us -> 103 us
    pallas_call x1, Pallas kernels: 106 us -> 103 us  [local(): pl.pallas_call(functools.partial(kernel, chips), name='layer', out_shape=...]
where the time goes in v2:
time: 105 us
  Pallas kernels  103 us (98%)
  local copies, waits for them, and re-layouts  2.02 us (2%)
    pallas_call x1, Pallas kernels, local(): pl.pallas_call(functools.partial(kernel, chips), name='layer', out_shape=...  103 us

profile of v2, /device:TPU:0, one launch (start us, length us, event | category | flops | bytes accessed | tf_op | source)
XLA Modules:
  0.0 105.2 jit_solution(12115690747730997193)
XLA Ops:
  0.0 103.2 %layer.1 = bf16[8,8,32,1024]{3,2,1,0:T(8,128)(2,1)S(1)} custom-call(bf16[8,8,32,1024]{3,2,1,0:T(8,128)(2,1)} %bitcast.4, bf16[512,129]{1,0:T(8,128)(2,1)} %bitcast.5, bf16[64,64]{1,0:T(8,128)(2,1)} %mix_weight.1, f32[64]{0:T(128)} %channel_bias.1), custom_call_target="tpu_custom_call" | custom-call | tf_op jit(solution)/shard_map/layer/pallas_call | solution.py:410
  103.2 2.0 %copy.6 = bf16[64,32,1024]{2,1,0:T(8,128)(2,1)} copy(bf16[64,32,1024]{2,1,0:T(8,128)(2,1)S(1)} %bitcast.3) | data formatting | bytes 8388608

commit v3 on v2

--- a/solution.py
+++ b/solution.py
@@ -35,6 +35,7 @@
     total,
     staged,
     stage,
+    stage_wrap,
     load_sem,
     param_sem,
     own_send,
@@ -49,6 +50,12 @@
     hop_send,
     hop_recv,
     ready,
+    ready_wrap,
+    late_send,
+    wrap_send,
+    wrap_recv,
+    wrap_pass,
+    wrap_done,
 ):
     groups, width, strip_rows, columns = features.shape
     _, _, _, pieces, _, _, piece = halo.shape
@@ -72,6 +79,9 @@
     up_chip = lax.rem(chip + 2, chips)
     down_chip = lax.rem(chip + chips - 2, chips)
     last = (groups - 1, pieces - 1)
+    late = (groups - 1, pieces - 2)
+    front = pl.ds(0, width // 2)
+    rear = pl.ds(width // 2, width // 2)
 
     def half(which):
         return pl.ds(pl.multiple_of(which * part, part), part)
@@ -110,7 +120,7 @@
         return pltpu.make_async_remote_copy(
             src_ref=halo.at[1 - odd, t, g, q],
             dst_ref=halo.at[odd, t, g, q],
-            send_sem=far_send,
+            send_sem=far_send.at[g],
             recv_sem=far_recv.at[g, q, turn],
             device_id=(far,),
             device_id_type=MESH,
@@ -141,11 +151,53 @@
         return pltpu.make_async_remote_copy(
             src_ref=stage.at[turn],
             dst_ref=halo.at[1 - odd, 1 - core if turn else core, *last],
-            send_sem=far_send,
+            send_sem=far_send.at[last[0]],
             recv_sem=far_recv.at[*last, turn],
             device_id=(near[0],),
             device_id_type=MESH,
         )
+
+    def late_copy(turn, part_rows):
+        t = 1 - core if turn else core
+        return pltpu.make_async_remote_copy(
+            src_ref=halo.at[1 - odd, t, *late, part_rows],
+            dst_ref=halo.at[odd, t, *late, part_rows],
+            send_sem=late_send,
+            recv_sem=far_recv.at[*late, turn],
+            device_id=(far,),
+            device_id_type=MESH,
+        )
+
+    def wrap_copy(turn):
+        return pltpu.make_async_remote_copy(
+            src_ref=other.at[*late, front] if turn else own.at[core, *late, front],
+            dst_ref=stage_wrap.at[turn],
+            send_sem=wrap_send,
+            recv_sem=wrap_recv.at[turn],
+            device_id=(back[turn],),
+            device_id_type=MESH,
+        )
+
+    def wrap_forward(turn):
+        return pltpu.make_async_remote_copy(
+            src_ref=stage_wrap.at[turn],
+            dst_ref=halo.at[1 - odd, 1 - core if turn else core, *late, front],
+            send_sem=wrap_pass,
+            recv_sem=wrap_done.at[turn],
+            device_id=(near[0],),
+            device_id_type=MESH,
+        )
+
+    def wrap_arrived(turn):
+        region = halo.at[odd, 1 - core if turn else core, *late, front]
+        pltpu.make_async_remote_copy(
+            src_ref=region,
+            dst_ref=region,
+            send_sem=wrap_pass,
+            recv_sem=wrap_done.at[turn],
+            device_id=(near[0],),
+            device_id_type=MESH,
+        ).wait_recv()
 
     def send_near(g):
         for q in range(pieces):
@@ -155,10 +207,14 @@
     def relay(g, q):
         for turn in range(2):
             near_wait(g, q, turn)
-            if q < last[1]:
+            if q < late[1]:
                 far_copy(g, q, turn).start()
-            else:
-                pl.when(g < last[0])(far_copy(g, q, turn).start)
+                continue
+            pl.when(g < last[0])(far_copy(g, q, turn).start)
+            if q == late[1]:
+                final = g == last[0]
+                pl.when(final & (chip != chips - 2))(late_copy(turn, pl.ds(0, width)).start)
+                pl.when(final & (chip == chips - 2))(late_copy(turn, rear).start)
 
     def dot(a, b):
         return jnp.dot(a, b, preferred_element_type=jnp.float32)
@@ -230,12 +286,21 @@
                     value += dot(mixer[:, pl.ds(i * block, block)], wide(own.at[b, i], n * PAIR, PAIR))
                 total[slot, b, :, pl.ds(n * span, span)] = value
 
-    def outer(g, first, count):
+    def outer(g, first, count, tail=False):
         slot = lax.rem(g, 2)
         cols = pl.ds(first * piece, count * piece)
         for q in range(first, first + count):
             for turn in range(2):
-                far_copy(g, q, turn).wait_recv()
+                if not tail or q != late[1]:
+                    far_copy(g, q, turn).wait_recv()
+                    continue
+                pl.when(chip > 0)(far_copy(g, q, turn).wait_recv)
+
+                @pl.when(chip == 0)
+                def _():
+                    late_copy(turn, rear).wait_recv()
+                    wrap_arrived(turn)
+
         for b in range(CORES):
             value = total[slot, b, :, cols]
             for role in range(2):
@@ -260,16 +325,17 @@
     load(0)
     load(groups - 1)
     barrier = pltpu.get_barrier_semaphore()
-    close = (*near, peer, down_chip * CORES, down_chip * CORES + 1)
+    def signal(sem, devices):
+        for device in devices:
+            pl.semaphore_signal(sem, inc=1, device_id=(device,), device_id_type=MESH)
+
+    close = (*near, peer)
     above = (up_chip * CORES, up_chip * CORES + 1)
-    for friend in close:
-        pl.semaphore_signal(barrier, inc=1, device_id=(friend,), device_id_type=MESH)
-
-    @pl.when(chip < chips - 2)
-    def _():
-        for friend in above:
-            pl.semaphore_signal(barrier, inc=1, device_id=(friend,), device_id_type=MESH)
-
+    below = (down_chip * CORES, down_chip * CORES + 1)
+    first_chips, last_chips = chip < 2, chip >= chips - 2
+    signal(barrier, close)
+    pl.when(jnp.logical_not(last_chips))(lambda: signal(barrier, above))
+    pl.when(first_chips)(lambda: signal(barrier, below))
     raw_copy = pltpu.make_async_copy(row_kernel, raw, param_sem.at[0])
     mix_copy = pltpu.make_async_copy(mix_weight, raw_mix, param_sem.at[1])
     bias_copy = pltpu.make_async_copy(channel_bias, bias, param_sem.at[2])
@@ -278,13 +344,16 @@
     raw_copy.start()
     mix_copy.start()
     bias_copy.start()
-    pl.semaphore_wait(barrier, len(close) + len(above) * jnp.minimum(lax.div(chip, 2), 1))
-
-    @pl.when(chip >= chips - 2)
-    def _():
-        for friend in above:
-            pl.semaphore_signal(ready, inc=1, device_id=(friend,), device_id_type=MESH)
-
+    inner_chip = jnp.minimum(lax.div(chip, 2), 1)
+    final_chip = lax.div(chip + 2, chips)
+    pl.semaphore_wait(barrier, len(close) + len(below) * inner_chip + len(above) * final_chip)
+    pl.when(jnp.logical_not(first_chips))(lambda: signal(ready, below))
+    pl.when(last_chips)(lambda: signal(ready_wrap, above))
+
+    def wait_above():
+        @pl.when(jnp.logical_not(last_chips))
+        def _():
+            pl.semaphore_wait(ready, len(above))
 
     def hop():
         for turn in range(2):
@@ -293,7 +362,14 @@
     loaded(0)
     send_near(0)
     loaded(groups - 1)
+    pl.when(odd == 1)(wait_above)
     pl.when(chip > 0)(hop)
+
+    @pl.when(chip == chips - 1)
+    def _():
+        for turn in range(2):
+            wrap_copy(turn).start()
+
     for g in range(1, AHEAD):
         loaded(g)
         send_near(g)
@@ -311,14 +387,16 @@
         device_id_type=MESH,
     ).wait_recv()
 
+    pl.when(odd == 0)(wait_above)
+
     @pl.when(chip == 1)
     def _():
-        pl.semaphore_wait(ready, len(above))
+        pl.semaphore_wait(ready_wrap, len(below))
 
     def step(g, carry):
         @pl.when((g == 1) & (chip == 0))
         def _():
-            pl.semaphore_wait(ready, len(above))
+            pl.semaphore_wait(ready_wrap, len(below))
             hop()
 
         @pl.when(g == groups - 1)
@@ -327,6 +405,12 @@
                 hop_copy(turn).wait_recv()
                 hop_forward(turn).start()
 
+            @pl.when(chip == 1)
+            def _():
+                for turn in range(2):
+                    wrap_copy(turn).wait_recv()
+                    wrap_forward(turn).start()
+
         @pl.when(g + AHEAD < groups)
         def _():
             send_near(g + AHEAD)
@@ -360,7 +444,7 @@
 
     lax.fori_loop(0, groups, step, 0)
     for q in reversed(range(PAIR, pieces)):
-        outer(groups - 1, q, 1)
+        outer(groups - 1, q, 1, tail=True)
 
     def sent(ref, sem):
         pltpu.make_async_remote_copy(
@@ -374,7 +458,13 @@
 
     sent(other, own_send)
     sent(features, near_send)
-    sent(halo.at[0], far_send)
+    for g in range(groups - 1):
+        sent(halo.at[0, :, g], far_send.at[g])
+    sent(halo.at[0, :, last[0], pl.ds(0, last[1])], far_send.at[last[0]])
+    pl.when(chip != chips - 2)(lambda: sent(stage, late_send))
+    pl.when(chip == chips - 2)(lambda: sent(stage_wrap, late_send))
+    pl.when(chip == chips - 1)(lambda: sent(stage_wrap, wrap_send))
+    pl.when(chip == 1)(lambda: sent(stage_wrap, wrap_pass))
     sent(stage, hop_send)
     pltpu.make_async_copy(staged.at[core], out.at[:, :, :, half(core)], out_sem).wait()
     swapped = pltpu.make_async_remote_copy(
@@ -428,13 +518,14 @@
             pltpu.VMEM((2, CORES, block, part), jnp.float32),
             pltpu.VMEM((CORES, groups, width, strip_rows, part), bf16),
             pltpu.VMEM((2, width, strip_rows, LANES), bf16),
+            pltpu.VMEM((2, width // 2, strip_rows, LANES), bf16),
             dma((groups,)),
             dma((3,)),
             dma,
             dma,
             dma,
             dma((groups, pieces, CORES)),
-            dma,
+            dma((groups,)),
             dma((groups, pieces, CORES)),
             dma,
             dma,
@@ -442,6 +533,12 @@
             dma,
             dma((2,)),
             pltpu.SemaphoreType.REGULAR,
+            pltpu.SemaphoreType.REGULAR,
+            dma,
+            dma,
+            dma((2,)),
+            dma,
+            dma((2,)),
         ],
         compiler_params=pltpu.CompilerParams(
             collective_id=0, has_side_effects=True, vmem_limit_bytes=48 * 1024 * 1024

time: 105 us -> 104 us (level)
    pallas_call x1, Pallas kernels: 103 us -> 102 us  [local(): pl.pallas_call(functools.partial(kernel, chips), name='layer', out_shape=...]
where the time goes in v3:
time: 104 us
  Pallas kernels  102 us (98%)
  local copies, waits for them, and re-layouts  2.02 us (2%)
    pallas_call x1, Pallas kernels, local(): pl.pallas_call(functools.partial(kernel, chips), name='layer', out_shape=...  102 us

profile of v3, /device:TPU:0, one launch (start us, length us, event | category | flops | bytes accessed | tf_op | source)
XLA Modules:
  0.0 103.9 jit_solution(849987071363107681)
XLA Ops:
  0.0 101.9 %layer.1 = bf16[8,8,32,1024]{3,2,1,0:T(8,128)(2,1)S(1)} custom-call(bf16[8,8,32,1024]{3,2,1,0:T(8,128)(2,1)} %bitcast.4, bf16[512,129]{1,0:T(8,128)(2,1)} %bitcast.5, bf16[64,64]{1,0:T(8,128)(2,1)} %mix_weight.1, f32[64]{0:T(128)} %channel_bias.1), custom_call_target="tpu_custom_call" | custom-call | tf_op jit(solution)/shard_map/layer/pallas_call | solution.py:500
  101.9 2.0 %copy.6 = bf16[64,32,1024]{2,1,0:T(8,128)(2,1)} copy(bf16[64,32,1024]{2,1,0:T(8,128)(2,1)S(1)} %bitcast.3) | data formatting | bytes 8388608

commit v4 on v3

--- a/solution.py
+++ b/solution.py
@@ -301,18 +301,17 @@
                     late_copy(turn, rear).wait_recv()
                     wrap_arrived(turn)
 
-        for b in range(CORES):
+        place = pl.ds(pl.multiple_of(core * part + first * piece, piece), count * piece)
+
+        def finish(b):
             value = total[slot, b, :, cols]
-            for role in range(2):
-                for t in range(CORES):
-                    s = t + (2 * CORES if role else 0) - b
-                    if 0 <= s < segments:
-                        value += dot(weights[lax.rem(g, 3), s], wide(halo.at[role, t, g], first, count))
+            for role, t, s in ((0, b, 0), (b, 1 - b, 1 + b * (segments - 3)), (1, b, segments - 1)):
+                value += dot(weights[lax.rem(g, 3), s], wide(halo.at[role, t, g], first, count))
             for o in range(width):
                 x = value[o * strip_rows : (o + 1) * strip_rows] + bias[g * width + o]
                 staged[b, g, o, :, cols] = jax.nn.gelu(x).astype(jnp.bfloat16)
-        place = pl.ds(pl.multiple_of(core * part + first * piece, piece), count * piece)
-        pltpu.make_async_copy(staged.at[core, g, :, :, cols], out.at[g, :, :, place], out_sem).start()
+
+        finish(1 - core)
         pltpu.make_async_remote_copy(
             src_ref=staged.at[1 - core, g, :, :, cols],
             dst_ref=out.at[g, :, :, place],
@@ -321,6 +320,8 @@
             device_id=(peer,),
             device_id_type=MESH,
         ).start()
+        finish(core)
+        pltpu.make_async_copy(staged.at[core, g, :, :, cols], out.at[g, :, :, place], out_sem).start()
 
     load(0)
     load(groups - 1)
@@ -399,6 +400,29 @@
             pl.semaphore_wait(ready_wrap, len(below))
             hop()
 
+        @pl.when(g + AHEAD < groups)
+        def _():
+            send_near(g + AHEAD)
+
+        relay(g, 0)
+
+        @pl.when(g == 0)
+        def _():
+            build(g)
+            inner(g)
+
+        @pl.when(g + 1 < groups)
+        def _():
+            build(g + 1)
+
+        relay(g, 1)
+
+        @pl.when(g > 0)
+        def _():
+            outer(g - 1, PAIR, PAIR)
+
+        relay(g, 2)
+
         @pl.when(g == groups - 1)
         def _():
             for turn in range(2):
@@ -410,29 +434,6 @@
                 for turn in range(2):
                     wrap_copy(turn).wait_recv()
                     wrap_forward(turn).start()
-
-        @pl.when(g + AHEAD < groups)
-        def _():
-            send_near(g + AHEAD)
-
-        relay(g, 0)
-
-        @pl.when(g == 0)
-        def _():
-            build(g)
-            inner(g)
-
-        @pl.when(g + 1 < groups)
-        def _():
-            build(g + 1)
-
-        relay(g, 1)
-
-        @pl.when(g > 0)
-        def _():
-            outer(g - 1, PAIR, PAIR)
-
-        relay(g, 2)
 
         @pl.when(g + 1 < groups)
         def _():

time: 104 us -> 104 us (level)
  no operation moved by 1% of the time
where the time goes in v4:
time: 104 us
  Pallas kernels  102 us (98%)
  local copies, waits for them, and re-layouts  2.02 us (2%)
    pallas_call x1, Pallas kernels, local(): pl.pallas_call(functools.partial(kernel, chips), name='layer', out_shape=...  102 us

profile of v4, /device:TPU:0, one launch (start us, length us, event | category | flops | bytes accessed | tf_op | source)
XLA Modules:
  0.0 104.0 jit_solution(17597485038103432433)
XLA Ops:
  0.0 101.9 %layer.1 = bf16[8,8,32,1024]{3,2,1,0:T(8,128)(2,1)S(1)} custom-call(bf16[8,8,32,1024]{3,2,1,0:T(8,128)(2,1)} %bitcast.4, bf16[512,129]{1,0:T(8,128)(2,1)} %bitcast.5, bf16[64,64]{1,0:T(8,128)(2,1)} %mix_weight.1, f32[64]{0:T(128)} %channel_bias.1), custom_call_target="tpu_custom_call" | custom-call | tf_op jit(solution)/shard_map/layer/pallas_call | solution.py:501
  101.9 2.0 %copy.6 = bf16[64,32,1024]{2,1,0:T(8,128)(2,1)} copy(bf16[64,32,1024]{2,1,0:T(8,128)(2,1)S(1)} %bitcast.3) | data formatting | bytes 8388608

commit v5 on v3

--- a/solution.py
+++ b/solution.py
@@ -411,11 +411,11 @@
                     wrap_copy(turn).wait_recv()
                     wrap_forward(turn).start()
 
+        relay(g, 0)
+
         @pl.when(g + AHEAD < groups)
         def _():
             send_near(g + AHEAD)
-
-        relay(g, 0)
 
         @pl.when(g == 0)
         def _():

time: 104 us -> 104 us (level)
  no operation moved by 1% of the time
where the time goes in v5:
time: 104 us
  Pallas kernels  102 us (98%)
  local copies, waits for them, and re-layouts  2.02 us (2%)
    pallas_call x1, Pallas kernels, local(): pl.pallas_call(functools.partial(kernel, chips), name='layer', out_shape=...  102 us

profile of v5, /device:TPU:0, one launch (start us, length us, event | category | flops | bytes accessed | tf_op | source)
XLA Modules:
  0.0 103.9 jit_solution(431884169923255220)
XLA Ops:
  0.0 101.9 %layer.1 = bf16[8,8,32,1024]{3,2,1,0:T(8,128)(2,1)S(1)} custom-call(bf16[8,8,32,1024]{3,2,1,0:T(8,128)(2,1)} %bitcast.4, bf16[512,129]{1,0:T(8,128)(2,1)} %bitcast.5, bf16[64,64]{1,0:T(8,128)(2,1)} %mix_weight.1, f32[64]{0:T(128)} %channel_bias.1), custom_call_target="tpu_custom_call" | custom-call | tf_op jit(solution)/shard_map/layer/pallas_call | solution.py:500
  101.9 2.0 %copy.6 = bf16[64,32,1024]{2,1,0:T(8,128)(2,1)} copy(bf16[64,32,1024]{2,1,0:T(8,128)(2,1)S(1)} %bitcast.3) | data formatting | bytes 8388608
